TPU v7x, 32 devices: a whole 2x2x4 slice. The times are simulated.
32 devices in a mesh: rep: 4 (over x, y), dp: 8 (over z, core).
Axes of the slice: x: 2, y: 2, z: 4, core: 2. Of those that a mesh axis runs over, the one named last changes fastest.
Arguments:
- x: bfloat16 [32, 4096, 768], P(('rep', 'dp')), parts along dimension 0
- dy: bfloat16 [32, 4096, 768], P(('rep', 'dp')), parts along dimension 0
- w_gate: bfloat16 [2, 768, 2304], P(None, 'dp')
- w_up: bfloat16 [2, 768, 2304], P(None, 'dp')
- w_down: bfloat16 [2, 2304, 768], P(None, 'dp')
- m_w_gate: float32 [2, 768, 2304], P(None, 'dp')
- m_w_up: float32 [2, 768, 2304], P(None, 'dp')
- m_w_down: float32 [2, 2304, 768], P(None, 'dp')
- v_w_gate: float32 [2, 768, 2304], P(None, 'dp')
- v_w_up: float32 [2, 768, 2304], P(None, 'dp')
- v_w_down: float32 [2, 2304, 768], P(None, 'dp')
Outputs:
- output 1: bfloat16 [8, 768, 2304], P('rep', 'dp'), parts along dimension 0
- output 2: bfloat16 [8, 768, 2304], P('rep', 'dp'), parts along dimension 0
- output 3: bfloat16 [8, 2304, 768], P('rep', 'dp'), parts along dimension 0
- output 4: float32 [8, 768, 2304], P('rep', 'dp'), parts along dimension 0
- output 5: float32 [8, 768, 2304], P('rep', 'dp'), parts along dimension 0
- output 6: float32 [8, 2304, 768], P('rep', 'dp'), parts along dimension 0
- output 7: float32 [8, 768, 2304], P('rep', 'dp'), parts along dimension 0
- output 8: float32 [8, 768, 2304], P('rep', 'dp'), parts along dimension 0
- output 9: float32 [8, 2304, 768], P('rep', 'dp'), parts along dimension 0
There are 4 independent parts. A program takes and returns all parts, laid end to end along the dimension named above; an argument that names none is the same for every part.
All inputs are finite; a program needn't handle non-finite values.
Results may differ from a plain program's by a relative error of at most 0.022.
Values are sent between devices in bfloat16 or wider.
A program may use at most 2 GiB of HBM per device.

v0:
```python
import jax
import jax.numpy as jnp
from jax import lax
from jax.sharding import PartitionSpec as P

NAMES = ("w_gate", "w_up", "w_down")


def matmul(a, w):
    return jnp.dot(a, w, preferred_element_type=jnp.float32).astype(jnp.bfloat16)


def normed(h):
    wide = h.astype(jnp.float32)
    scale = lax.rsqrt(jnp.mean(wide**2, -1, keepdims=True) + 1e-6)
    return (wide * scale).astype(jnp.bfloat16)


def layer(h, w):
    a = normed(h)
    gate = jnp.dot(a, w["w_gate"], preferred_element_type=jnp.float32)
    up = jnp.dot(a, w["w_up"], preferred_element_type=jnp.float32)
    return h + matmul((jax.nn.silu(gate) * up).astype(jnp.bfloat16), w["w_down"])


def adamw(w, m, v, g):
    m = 0.9 * m + 0.1 * g
    v = 0.95 * v + 0.05 * g * g
    step = m * lax.rsqrt(v + 1e-8) + 0.1 * w
    return (w - 0.02 * step).astype(jnp.bfloat16), m, v


def clipped(gradients, sum_of_squares, count):
    factor = jnp.minimum(1.0, 0.5 * lax.rsqrt(sum_of_squares / count + 1e-30))
    return [g * factor for g in gradients]


def solution(mesh):
    def fetched(weights, number):
        return {name: lax.all_gather(w[number], "dp", axis=0, tiled=True) for name, w in zip(NAMES, weights, strict=True)}

    def step(x, dy, *arrays):
        weights, m, v = (arrays[i : i + 3] for i in (0, 3, 6))
        layers = weights[0].shape[0]
        h, kept = x[0], []
        for number in range(layers):
            kept.append(h)
            h = layer(h, fetched(weights, number))
        by_h, mine = dy[0], [None] * layers
        for number in reversed(range(layers)):
            _, back = jax.vjp(lambda w, h: layer(h, w), fetched(weights, number), kept[number])
            by_w, by_h = back(by_h)
            mine[number] = [lax.psum_scatter(by_w[name], "dp", scatter_dimension=0, tiled=True) for name in NAMES]
        gradients = [jnp.stack([mine[number][i] for number in range(layers)]).astype(jnp.float32) for i in range(3)]
        squares = lax.psum(sum(jnp.sum(g * g) for g in gradients), "dp")
        gradients = clipped(gradients, squares, lax.psum(1, "dp") * sum(g.size for g in gradients))
        new = [adamw(w.astype(jnp.float32), m, v, g) for w, m, v, g in zip(weights, m, v, gradients, strict=True)]
        return tuple(one[which] for which in range(3) for one in new)

    states, cut = P(("rep", "dp"), None, None), P(None, "dp", None)
    return jax.shard_map(
        step,
        mesh=mesh,
        in_specs=(states, states) + (cut,) * 9,
        out_specs=(P("rep", "dp", None),) * 9,
        check_vma=False,
    )
```

profile of v0, /device:TPU:0, one launch (start us, length us, event | category | flops | bytes accessed | tf_op | source)
XLA Modules:
  0.0 704.2 jit_solution(2461806448373662176)
XLA Ops:
  28.3 8.8 %copy.21 = bf16[1,4096,768]{1,2,0:T(8,128)(2,1)} copy(bf16[1,4096,768]{2,1,0:T(8,128)(2,1)} %param.12) | data formatting | bytes 12582912 | tf_op args[1]
  37.1 17.0 %all-gather.13.cloned.1.call-done = bf16[1,768,2304]{2,1,0:T(8,128)(2,1)} async-done(((bf16[1,96,2304]{2,1,0:T(8,128)(2,1)}), bf16[1,768,2304]{2,1,0:T(8,128)(2,1)}) %all-gather.13.cloned.1.call-update) | async-done | bytes 3538960 | tf_op jit(solution)/shard_map/all_gather | solution.py:40
  54.1 23.6 %fusion.46 = f32[4096,2304]{1,0:T(8,128)} fusion(bf16[1,4096,768]{1,2,0:T(8,128)(2,1)} %copy.20, f32[4096]{0:T(1024)S(1)} %add_rsqrt_fusion, bf16[1,768,2304]{2,1,0:T(8,128)(2,1)} %all-gather.13.cloned.1.call-done), kind=kOutput, calls=%fused_computation.57 | convolution fusion | flops 14504951808 | bytes 47595520 | tf_op jit(solution)/shard_map/dot_general | solution.py:21
  77.6 18.9 %all-gather.15.cloned.1.call-done = bf16[1,768,2304]{2,1,0:T(8,128)(2,1)} async-done(((bf16[1,96,2304]{2,1,0:T(8,128)(2,1)}), bf16[1,768,2304]{2,1,0:T(8,128)(2,1)}) %all-gather.15.cloned.1.call-update) | async-done | bytes 3538960 | tf_op jit(solution)/shard_map/all_gather | solution.py:40
  96.6 37.9 %multiply_convert_fusion.1 = (bf16[4096,2304]{1,0:T(8,128)(2,1)}, f32[4096,2304]{1,0:T(8,128)}) fusion(f32[4096,2304]{1,0:T(8,128)} %fusion.46, bf16[1,768,2304]{2,1,0:T(8,128)(2,1)} %all-gather.15.cloned.1.call-done, bf16[1,4096,768]{1,2,0:T(8,128)(2,1)} %copy.20, f32[4096]{0:T(1024)S(1)} %add_rsqrt_fusion), kind=kOutput, calls=%fused_computation.17 | convolution fusion | flops 14561574912 | bytes 104218624 | tf_op jit(solution)/shard_map/dot_general | solution.py:22
  139.1 23.8 %fusion.19 = (f32[4096]{0:T(1024)S(1)}, bf16[4096,768]{0,1:T(8,128)(2,1)}) fusion(bf16[4096,2304]{1,0:T(8,128)(2,1)} %get-tuple-element.24, bf16[1,2304,768]{2,1,0:T(8,128)(2,1)} %all-gather.17.cloned.1.call-done, bf16[1,4096,768]{1,2,0:T(8,128)(2,1)} %copy.20), kind=kOutput, calls=%fused_computation.37 | convolution fusion | flops 14511239168 | bytes 35012608 | tf_op jit(solution)/shard_map/dot_general | solution.py:10
  163.5 17.9 %all-gather.21.cloned.1.call-done = bf16[1,2304,768]{2,1,0:T(8,128)(2,1)} async-done(((bf16[1,288,768]{2,1,0:T(8,128)(2,1)}), bf16[1,2304,768]{2,1,0:T(8,128)(2,1)}) %all-gather.21.cloned.1.call-update) | async-done | bytes 3538960 | tf_op jit(solution)/shard_map/all_gather | solution.py:40
  181.4 21.6 %convolution_convert_fusion.1 = bf16[4096,2304]{1,0:T(8,128)(2,1)} fusion(bf16[1,4096,768]{2,1,0:T(8,128)(2,1)} %param.12, bf16[1,2304,768]{2,1,0:T(8,128)(2,1)} %all-gather.21.cloned.1.call-done), kind=kOutput, calls=%fused_computation.23 | convolution fusion | flops 14504951808 | bytes 28704768 | tf_op jit(solution)/shard_map/transpose(jvp())/dot_general | solution.py:10
  203.0 20.7 %all-gather.23.cloned.1.call-done = bf16[1,768,2304]{2,1,0:T(8,128)(2,1)} async-done(((bf16[1,96,2304]{2,1,0:T(8,128)(2,1)}), bf16[1,768,2304]{2,1,0:T(8,128)(2,1)}) %all-gather.23.cloned.1.call-update) | async-done | bytes 3538960 | tf_op jit(solution)/shard_map/all_gather | solution.py:40
  223.7 23.5 %fusion.38 = f32[4096,2304]{1,0:T(8,128)} fusion(bf16[4096,768]{0,1:T(8,128)(2,1)} %get-tuple-element.27, f32[4096]{0:T(1024)S(1)} %fusion.78, bf16[1,768,2304]{2,1,0:T(8,128)(2,1)} %all-gather.23.cloned.1.call-done), kind=kOutput, calls=%fused_computation.54 | convolution fusion | flops 14504951808 | bytes 47595520 | tf_op jit(solution)/shard_map/jvp()/dot_general | solution.py:22
  247.2 18.8 %all-gather.19.cloned.1.call-done = bf16[1,768,2304]{2,1,0:T(8,128)(2,1)} async-done(((bf16[1,96,2304]{2,1,0:T(8,128)(2,1)}), bf16[1,768,2304]{2,1,0:T(8,128)(2,1)}) %all-gather.19.cloned.1.call-update) | async-done | bytes 3538960 | tf_op jit(solution)/shard_map/all_gather | solution.py:40
  266.1 51.7 %fusion.2 = (bf16[4096,2304]{1,0:T(8,128)(2,1)}, f32[4096,2304]{1,0:T(8,128)}) fusion(f32[4096,2304]{1,0:T(8,128)} %fusion.38, bf16[4096,2304]{1,0:T(8,128)(2,1)} %convolution_convert_fusion.1, bf16[1,768,2304]{2,1,0:T(8,128)(2,1)} %all-gather.19.cloned.1.call-done, bf16[4096,768]{0,1:T(8,128)(2,1)} %get-tuple-element.27, f32[4096]{0:T(1024)S(1)} %fusion.78), kind=kOutput, calls=%fused_computation.8 | convolution fusion | flops 14618198016 | bytes 123092992 | tf_op jit(solution)/shard_map/jvp()/dot_general | solution.py:21
  317.8 21.5 %convolution_convert_fusion.2 = bf16[4096,768]{0,1:T(8,128)(2,1)} fusion(bf16[4096,2304]{1,0:T(8,128)(2,1)} %get-tuple-element.28, bf16[1,768,2304]{2,1,0:T(8,128)(2,1)} %all-gather.19.cloned.1.call-done), kind=kOutput, calls=%fused_computation.41 | convolution fusion | flops 14495514624 | bytes 28704768 | tf_op jit(solution)/shard_map/transpose(jvp())/dot_general | solution.py:21
  339.3 28.3 %fusion.21 = (f32[4096]{0:T(1024)S(1)}, bf16[4096,768]{0,1:T(8,128)(2,1)}) fusion(bf16[4096,768]{0,1:T(8,128)(2,1)} %get-tuple-element.27, bf16[4096,768]{0,1:T(8,128)(2,1)} %convolution_convert_fusion.2, bf16[1,768,2304]{2,1,0:T(8,128)(2,1)S(1)} %copy-done.18, bf16[4096,2304]{1,0:T(8,128)(2,1)} %convolution_convert_fusion.1, ...), kind=kOutput, calls=%fused_computation.39 | convolution fusion | flops 14571008000 | bytes 79052800 | tf_op jit(solution)/shard_map/transpose(jvp())/dot_general | solution.py:22
  378.3 19.5 %convolution_convert_fusion.5 = bf16[2304,768]{1,0:T(8,128)(2,1)} fusion(bf16[4096,2304]{1,0:T(8,128)(2,1)} %get-tuple-element.24, bf16[4096,768]{0,1:T(8,128)(2,1)S(1)} %fusion.24), kind=kOutput, calls=%fused_computation.53 | convolution fusion | flops 14497284096 | bytes 28704768 | tf_op jit(solution)/shard_map/transpose(jvp())/dot_general | solution.py:10
  397.8 32.2 %fusion.28 = bf16[2304,768]{1,0:T(8,128)(2,1)} fusion(bf16[1,4096,768]{2,1,0:T(8,128)(2,1)} %param.12, f32[4096,2304]{1,0:T(8,128)} %fusion.38, f32[4096,2304]{1,0:T(8,128)} %get-tuple-element.29), kind=kOutput, calls=%fused_computation.48 | convolution fusion | flops 14553907200 | bytes 85327872 | tf_op jit(solution)/shard_map/transpose(jvp())/dot_general | solution.py:10
  430.1 22.2 %convolution_convert_fusion = bf16[4096,2304]{1,0:T(8,128)(2,1)} fusion(bf16[4096,768]{0,1:T(8,128)(2,1)} %copy-done, bf16[1,2304,768]{2,1,0:T(8,128)(2,1)} %all-gather.17.cloned.1.call-done), kind=kOutput, calls=%fused_computation.22 | convolution fusion | flops 14504951808 | bytes 28704768 | tf_op jit(solution)/shard_map/transpose(jvp())/dot_general | solution.py:10
  452.3 27.8 %fusion.35 = bf16[768,2304]{1,0:T(8,128)(2,1)} fusion(bf16[4096,2304]{1,0:T(8,128)(2,1)} %convolution_convert_fusion, f32[4096,2304]{1,0:T(8,128)} %fusion.46, bf16[1,4096,768]{1,2,0:T(8,128)(2,1)} %copy.20, f32[4096]{0:T(1024)S(1)} %copy-done.17), kind=kOutput, calls=%fused_computation.51 | convolution fusion | flops 14563344384 | bytes 66469888 | tf_op jit(solution)/shard_map/transpose(jvp())/dot_general | solution.py:22
  480.2 28.1 %fusion.31 = bf16[768,2304]{1,0:T(8,128)(2,1)} fusion(bf16[4096,2304]{1,0:T(8,128)(2,1)} %convolution_convert_fusion.1, bf16[4096,768]{0,1:T(8,128)(2,1)} %get-tuple-element.27, f32[4096]{0:T(1024)S(1)} %copy-done.13, f32[4096,2304]{1,0:T(8,128)} %get-tuple-element.29), kind=kOutput, calls=%fused_computation.49 | convolution fusion | flops 14563344384 | bytes 66469888 | tf_op jit(solution)/shard_map/transpose(jvp())/dot_general | solution.py:22
  508.3 38.2 %fusion.32 = bf16[768,2304]{1,0:T(8,128)(2,1)} fusion(f32[4096,2304]{1,0:T(8,128)} %fusion.46, f32[4096,2304]{1,0:T(8,128)} %get-tuple-element.25, bf16[4096,2304]{1,0:T(8,128)(2,1)} %convolution_convert_fusion, bf16[1,4096,768]{1,2,0:T(8,128)(2,1)} %copy.20, f32[4096]{0:T(1024)S(1)} %copy-done.17), kind=kOutput, calls=%fused_computation.50 | convolution fusion | flops 14610530304 | bytes 104218624 | tf_op jit(solution)/shard_map/transpose(jvp())/dot_general | solution.py:21
  546.7 21.1 %convolution_convert_fusion.4 = bf16[768,2304]{1,0:T(8,128)(2,1)} fusion(bf16[4096,2304]{1,0:T(8,128)(2,1)} %get-tuple-element.28, bf16[4096,768]{0,1:T(8,128)(2,1)} %get-tuple-element.27, f32[4096]{0:T(1024)S(1)} %copy-done.13), kind=kOutput, calls=%fused_computation.52 | convolution fusion | flops 14504951808 | bytes 28721152 | tf_op jit(solution)/shard_map/transpose(jvp())/dot_general | solution.py:21
  578.3 42.9 %reduce-scatter.7.cloned.1.call-done = bf16[96,2304]{1,0:T(8,128)(2,1)} async-done(((bf16[768,2304]{1,0:T(8,128)(2,1)}), bf16[96,2304]{1,0:T(8,128)(2,1)}) %reduce-scatter.7.cloned.1.call-update) | async-done | bytes 442384 | tf_op jit(solution)/shard_map/reduce_scatter | solution.py:53
  621.3 45.1 %reduce-scatter.9.cloned.1.call-done = bf16[96,2304]{1,0:T(8,128)(2,1)} async-done(((bf16[768,2304]{1,0:T(8,128)(2,1)}), bf16[96,2304]{1,0:T(8,128)(2,1)}) %reduce-scatter.9.cloned.1.call-update) | async-done | bytes 442384 | tf_op jit(solution)/shard_map/reduce_scatter | solution.py:53
  670.5 15.0 %psum.7 = f32[]{:T(128)} all-reduce(f32[]{:T(128)S(6)} %add.99), channel_id=1, replica_groups=mesh['rep'=4,'dp'=8] {'dp'}, use_global_device_ids=true, to_apply=%region_12.13 | all-reduce | flops 1 | bytes 8 | tf_op jit(solution)/shard_map/psum | solution.py:55
  (81 shorter events, 60.5 us)
Async XLA Ops:
  7.2 46.9 %all-gather.13.cloned.1.call-start = ((), (), s32[]{:S(2)}) async-start(), calls=%async_computation.12 | async-start | bytes 3981312 | tf_op jit(solution)/shard_map/all_gather | solution.py:40
  9.4 87.2 %all-gather.15.cloned.1.call-start = ((), (), s32[]{:S(2)}) async-start(), calls=%async_computation.13 | async-start | bytes 3981312 | tf_op jit(solution)/shard_map/all_gather | solution.py:40
  11.5 127.5 %all-gather.17.cloned.1.call-start = ((), (), s32[]{:S(2)}) async-start(), calls=%async_computation.14 | async-start | bytes 3981312 | tf_op jit(solution)/shard_map/all_gather | solution.py:40
  13.7 167.6 %all-gather.21.cloned.1.call-start = ((), (), s32[]{:S(2)}) async-start(), calls=%async_computation.16 | async-start | bytes 3981312 | tf_op jit(solution)/shard_map/all_gather | solution.py:40
  14.3 209.4 %all-gather.23.cloned.1.call-start = ((), (), s32[]{:S(2)}) async-start(), calls=%async_computation.17 | async-start | bytes 3981312 | tf_op jit(solution)/shard_map/all_gather | solution.py:40
  14.9 251.2 %all-gather.19.cloned.1.call-start = ((), (), s32[]{:S(2)}) async-start(), calls=%async_computation.15 | async-start | bytes 3981312 | tf_op jit(solution)/shard_map/all_gather | solution.py:40
  15.5 552.4 %reduce-scatter.15.cloned.1.call-start = ((), (), s32[]{:S(2)}) async-start(), calls=%async_computation.10 | async-start | bytes 3981312 | tf_op jit(solution)/shard_map/reduce_scatter | solution.py:53
  28.3 68.3 %copy-start.16 = (f32[4096]{0:T(1024)}, f32[4096]{0:T(1024)S(1)}, u32[]{:S(2)}) copy-start(f32[4096]{0:T(1024)S(1)} %add_rsqrt_fusion) | copy-start | bytes 49156
  163.4 204.1 %copy-start.12 = (f32[4096]{0:T(1024)}, f32[4096]{0:T(1024)S(1)}, u32[]{:S(2)}) copy-start(f32[4096]{0:T(1024)S(1)} %fusion.78) | copy-start | bytes 49156
  317.8 21.5 %copy-start.18 = (bf16[1,768,2304]{2,1,0:T(8,128)(2,1)S(1)}, bf16[1,768,2304]{2,1,0:T(8,128)(2,1)}, u32[]{:S(2)}) copy-start(bf16[1,768,2304]{2,1,0:T(8,128)(2,1)} %all-gather.23.cloned.1.call-done) | copy-start | bytes 10616836
  339.3 28.3 %copy-start.15 = (f32[4096]{0:T(1024)S(1)}, f32[4096]{0:T(1024)}, u32[]{:S(2)}) copy-start(f32[4096]{0:T(1024)} %copy-done.14) | copy-start | bytes 49156
  397.7 170.1 %reduce-scatter.17.cloned.1.call-start = ((), (), s32[]{:S(2)}) async-start(), calls=%async_computation.11 | async-start | bytes 3981312 | tf_op jit(solution)/shard_map/reduce_scatter | solution.py:53
  430.1 22.2 %copy-start.17 = (f32[4096]{0:T(1024)S(1)}, f32[4096]{0:T(1024)}, u32[]{:S(2)}) copy-start(f32[4096]{0:T(1024)} %copy-done.16) | copy-start | bytes 49156
  430.1 140.2 %reduce-scatter.11.cloned.1.call-start = ((), (), s32[]{:S(2)}) async-start(), calls=%async_computation.8 | async-start | bytes 3981312 | tf_op jit(solution)/shard_map/reduce_scatter | solution.py:53
  452.3 27.9 %copy-start.13 = (f32[4096]{0:T(1024)S(1)}, f32[4096]{0:T(1024)}, u32[]{:S(2)}) copy-start(f32[4096]{0:T(1024)} %copy-done.12) | copy-start | bytes 49156
  480.1 96.0 %reduce-scatter.13.cloned.1.call-start = ((), (), s32[]{:S(2)}) async-start(), calls=%async_computation.9 | async-start | bytes 3981312 | tf_op jit(solution)/shard_map/reduce_scatter | solution.py:53
  508.3 113.0 %reduce-scatter.7.cloned.1.call-start = ((), (), s32[]{:S(2)}) async-start(), calls=%async_computation.6 | async-start | bytes 3981312 | tf_op jit(solution)/shard_map/reduce_scatter | solution.py:53
  546.6 119.8 %reduce-scatter.9.cloned.1.call-start = ((), (), s32[]{:S(2)}) async-start(), calls=%async_computation.7 | async-start | bytes 3981312 | tf_op jit(solution)/shard_map/reduce_scatter | solution.py:53
  567.8 118.4 %copy-start.1 = (bf16[2,288,768]{2,1,0:T(8,128)(2,1)S(1)}, bf16[2,288,768]{2,1,0:T(8,128)(2,1)}, u32[]{:S(2)}) copy-start(bf16[2,288,768]{2,1,0:T(8,128)(2,1)} %param.15) | copy-start | bytes 2654212
  567.8 123.5 %copy-start.2 = (bf16[2,96,2304]{2,1,0:T(8,128)(2,1)S(1)}, bf16[2,96,2304]{2,1,0:T(8,128)(2,1)}, u32[]{:S(2)}) copy-start(bf16[2,96,2304]{2,1,0:T(8,128)(2,1)} %param.13) | copy-start | bytes 2654212
  567.8 123.5 %copy-start.3 = (bf16[2,96,2304]{2,1,0:T(8,128)(2,1)S(1)}, bf16[2,96,2304]{2,1,0:T(8,128)(2,1)}, u32[]{:S(2)}) copy-start(bf16[2,96,2304]{2,1,0:T(8,128)(2,1)} %param.14) | copy-start | bytes 2654212
  570.2 121.1 %copy-start.4 = (bf16[96,2304]{1,0:T(8,128)(2,1)S(1)}, bf16[96,2304]{1,0:T(8,128)(2,1)}, u32[]{:S(2)}) copy-start(bf16[96,2304]{1,0:T(8,128)(2,1)} %reduce-scatter.11.cloned.1.call-done) | copy-start | bytes 1327108
  576.1 115.3 %copy-start.5 = (bf16[96,2304]{1,0:T(8,128)(2,1)S(1)}, bf16[96,2304]{1,0:T(8,128)(2,1)}, u32[]{:S(2)}) copy-start(bf16[96,2304]{1,0:T(8,128)(2,1)} %reduce-scatter.13.cloned.1.call-done) | copy-start | bytes 1327108
  686.3 6.2 copy-start.11
  (7 other events, 29.0 us)
Sparse Core Ops, SparseCore 0:
  10.2 43.8 all-gather.12
  56.3 40.2 all-gather.14
  98.8 40.2 all-gather.16
  141.1 40.2 all-gather.20
  183.4 40.2 all-gather.22
  225.8 40.2 all-gather.18
  397.9 42.6 reduce-scatter.14
  442.9 42.8 reduce-scatter.16
  488.1 42.8 reduce-scatter.10
  533.2 42.8 reduce-scatter.12
  578.4 42.8 reduce-scatter.6
  623.5 42.8 reduce-scatter.8
where the time goes:
time: 711 us; the launch traced here: 704 us
  matrix products  421 us (59%)
  waiting for transfers between devices  194 us (27%)
  other arithmetic  28.5 us (4%)
  local copies, waits for them, and re-layouts  28.2 us (4%)
  between operations  17.5 us (2%)
  blocking collectives  15 us (2%)
    dot_general x5, matrix products, layer(): gate = jnp.dot(a, w['w_gate'], preferred_element_type=jnp.float32)  156 us
    dot_general x5, matrix products, layer(): up = jnp.dot(a, w['w_up'], preferred_element_type=jnp.float32)  146 us
    dot_general x5, matrix products, matmul(): jnp.dot(a, w, preferred_element_type=jnp.float32).astype(jnp.bfloat16)  119 us
    all_gather x6, waiting for transfers between devices, fetched(): lax.all_gather(w[number], 'dp', axis=0, tiled=True)  97.9 us
    reduce_scatter x6, waiting for transfers between devices, step(): lax.psum_scatter(by_w[name], 'dp', scatter_dimension=0, tiled=True)  93.9 us
    unnamed x40, local copies, waits for them, and re-layouts  21.8 us
    psum x1, blocking collectives, step(): squares = lax.psum(sum((jnp.sum(g * g) for g in gradients)), 'dp')  15 us
  transfers between devices with their start and end apart: 12, of which 9 were waited for; matrix products, arithmetic and copies ran while one was open for 47% of the time, Pallas kernels for 0%

commit v1 on v0

v1 whole, which is shorter than its diff:
```python
import functools

import jax
import jax.numpy as jnp
from jax import lax
from jax.experimental import pallas as pl
from jax.experimental.pallas import tpu as pltpu
from jax.sharding import PartitionSpec as P

BF16, F32 = jnp.bfloat16, jnp.float32
VMEM_LIMIT = 62 * 2**20


def dot(a, b):
    return jnp.dot(a, b, preferred_element_type=F32)


def dot_t(a, b):
    return lax.dot_general(a, b, (((1,), (1,)), ((), ())), preferred_element_type=F32)


def t_dot(a, b):
    return lax.dot_general(a, b, (((0,), (0,)), ((), ())), preferred_element_type=F32)


def inverse_rms(wide):
    return lax.rsqrt(jnp.mean(wide * wide, -1, keepdims=True) + 1e-6)


def params(dims):
    return pltpu.CompilerParams(dimension_semantics=("arbitrary",) * dims, vmem_limit_bytes=VMEM_LIMIT)


def cost(units):
    return pl.CostEstimate(flops=int(units * 14.5e9), bytes_accessed=50_000_000, transcendentals=0)


def forward_kernel(nc, nt, x_ref, wg_ref, wu_ref, wd_ref, gate_ref, up_ref, a_out, h_out, a1_out, a_s, hid_s):
    c, t = pl.program_id(0), pl.program_id(1)
    tm = x_ref.shape[0]
    fc = wg_ref.shape[1]
    rows = pl.ds(pl.multiple_of(t * tm, tm), tm)

    @pl.when(c == 0)
    def _():
        wide = x_ref[...].astype(F32)
        a = (wide * inverse_rms(wide)).astype(BF16)
        a_s[rows, :] = a
        a_out[...] = a

    for k in range(nc):
        @pl.when(c == k)
        def _(k=k):
            a = a_s[rows, :]
            gate, up = dot(a, wg_ref[...]), dot(a, wu_ref[...])
            gate_ref[...] = gate
            up_ref[...] = up
            hid_s[rows, k * fc : (k + 1) * fc] = (gate * jax.nn.sigmoid(gate) * up).astype(BF16)

    @pl.when(c == nc)
    def _():
        h = x_ref[...] + dot(hid_s[rows, :], wd_ref[...]).astype(BF16)
        h_out[...] = h
        wide = h.astype(F32)
        a1_out[...] = (wide * inverse_rms(wide)).astype(BF16)


def forward(x, wg, wu, wd, tm=512, fc=768):
    tokens, d = x.shape
    ff = wg.shape[1]
    nc, nt = ff // fc, tokens // tm
    col = lambda c, t: (0, jnp.minimum(c, nc - 1))
    tile = lambda c, t: (jnp.where(c == nc, nt - 1, t), jnp.minimum(c, nc - 1))
    first = lambda c, t: (jnp.where(c == 0, t, nt - 1), 0)
    last = lambda c, t: (jnp.where(c == nc, t, 0), 0)
    return pl.pallas_call(
        functools.partial(forward_kernel, nc, nt),
        grid=(nc + 1, nt),
        in_specs=[
            pl.BlockSpec((tm, d), lambda c, t: (jnp.where((c == 0) | (c == nc), t, nt - 1), 0)),
            pl.BlockSpec((d, fc), col),
            pl.BlockSpec((d, fc), col),
            pl.BlockSpec((ff, d), lambda c, t: (0, 0), pipeline_mode=pl.Buffered(1)),
        ],
        out_specs=[pl.BlockSpec((tm, fc), tile), pl.BlockSpec((tm, fc), tile), pl.BlockSpec((tm, d), first), pl.BlockSpec((tm, d), last), pl.BlockSpec((tm, d), last)],
        out_shape=[jax.ShapeDtypeStruct((tokens, ff), F32)] * 2 + [jax.ShapeDtypeStruct((tokens, d), BF16)] * 3,
        scratch_shapes=[pltpu.VMEM((tokens, d), BF16), pltpu.VMEM((tokens, ff), BF16)],
        compiler_params=params(2),
        cost_estimate=cost(3),
        name="forward0",
    )(x, wg, wu, wd)


def hidden_grads(gate, up, dhid):
    dhid = dhid.astype(BF16).astype(F32)
    sig = jax.nn.sigmoid(gate)
    silu = gate * sig
    hid = (silu * up).astype(BF16)
    dup = (dhid * silu).astype(BF16)
    dgate = (dhid * up * (sig * (1 + gate * (1 - sig)))).astype(BF16)
    return hid, dgate, dup


def layer1_kernel(nt, a_ref, dy_ref, wg_ref, wu_ref, wd_ref, dwg_ref, dwu_ref, dwd_ref, dgate_ref, dup_ref, acg, acu, acd):
    t = pl.program_id(1)

    @pl.when(t == 0)
    def _():
        for acc in (acg, acu, acd):
            acc[...] = jnp.zeros_like(acc)

    a, dy = a_ref[...], dy_ref[...]
    hid, dgate, dup = hidden_grads(dot(a, wg_ref[...]), dot(a, wu_ref[...]), dot_t(dy, wd_ref[...]))
    dgate_ref[...] = dgate
    dup_ref[...] = dup
    acd[...] += t_dot(hid, dy)
    acg[...] += t_dot(a, dgate)
    acu[...] += t_dot(a, dup)

    @pl.when(t == nt - 1)
    def _():
        for out, acc in ((dwg_ref, acg), (dwu_ref, acu), (dwd_ref, acd)):
            out[...] = acc[...].astype(BF16)


def layer1(a, dy, wg, wu, wd, tm=1024, fc=768):
    tokens, d = a.shape
    ff = wg.shape[1]
    nc, nt = ff // fc, tokens // tm
    row, col, chunk, tile = (lambda c, t: (t, 0)), (lambda c, t: (0, c)), (lambda c, t: (c, 0)), (lambda c, t: (t, c))
    return pl.pallas_call(
        functools.partial(layer1_kernel, nt),
        grid=(nc, nt),
        in_specs=[pl.BlockSpec((tm, d), row)] * 2 + [pl.BlockSpec((d, fc), col)] * 2 + [pl.BlockSpec((fc, d), chunk)],
        out_specs=[pl.BlockSpec((d, fc), col)] * 2 + [pl.BlockSpec((fc, d), chunk)] + [pl.BlockSpec((tm, fc), tile)] * 2,
        out_shape=[jax.ShapeDtypeStruct((d, ff), BF16)] * 2 + [jax.ShapeDtypeStruct((ff, d), BF16)] + [jax.ShapeDtypeStruct((tokens, ff), BF16)] * 2,
        scratch_shapes=[pltpu.VMEM((d, fc), F32), pltpu.VMEM((d, fc), F32), pltpu.VMEM((fc, d), F32)],
        compiler_params=params(2),
        cost_estimate=cost(6),
        name="layer1",
    )(a, dy, wg, wu, wd)


def input_grad_kernel(dgate_ref, dup_ref, h_ref, dy_ref, wg_ref, wu_ref, out_ref):
    dn = (dot_t(dgate_ref[...], wg_ref[...]) + dot_t(dup_ref[...], wu_ref[...])).astype(BF16).astype(F32)
    wide = h_ref[...].astype(F32)
    scale = inverse_rms(wide)
    along = jnp.sum(dn * wide, -1, keepdims=True) * (scale * scale * scale) * (1.0 / wide.shape[-1])
    out_ref[...] = dy_ref[...] + (dn * scale - wide * along).astype(BF16)


def input_grad(dgate, dup, h, dy, wg, wu, tm=512):
    tokens, d = h.shape
    ff = wg.shape[1]
    row, whole = (lambda t: (t, 0)), (lambda t: (0, 0))
    return pl.pallas_call(
        input_grad_kernel,
        grid=(tokens // tm,),
        in_specs=[pl.BlockSpec((tm, ff), row)] * 2 + [pl.BlockSpec((tm, d), row)] * 2 + [pl.BlockSpec((d, ff), whole, pipeline_mode=pl.Buffered(1))] * 2,
        out_specs=pl.BlockSpec((tm, d), row),
        out_shape=jax.ShapeDtypeStruct((tokens, d), BF16),
        compiler_params=params(1),
        cost_estimate=cost(2),
        name="input_grad",
    )(dgate, dup, h, dy, wg, wu)


def layer0_kernel(nt, a_ref, dy_ref, gate_ref, up_ref, wd_ref, dwg_ref, dwu_ref, dwd_ref, acg, acu, acd):
    t = pl.program_id(1)

    @pl.when(t == 0)
    def _():
        for acc in (acg, acu, acd):
            acc[...] = jnp.zeros_like(acc)

    a, dy = a_ref[...], dy_ref[...]
    hid, dgate, dup = hidden_grads(gate_ref[...], up_ref[...], dot_t(dy, wd_ref[...]))
    acd[...] += t_dot(hid, dy)
    acg[...] += t_dot(a, dgate)
    acu[...] += t_dot(a, dup)

    @pl.when(t == nt - 1)
    def _():
        for out, acc in ((dwg_ref, acg), (dwu_ref, acu), (dwd_ref, acd)):
            out[...] = acc[...].astype(BF16)


def layer0(a, dy, gate, up, wd, tm=1024, fc=768):
    tokens, d = a.shape
    ff = wd.shape[0]
    nc, nt = ff // fc, tokens // tm
    row, col, chunk, tile = (lambda c, t: (t, 0)), (lambda c, t: (0, c)), (lambda c, t: (c, 0)), (lambda c, t: (t, c))
    return pl.pallas_call(
        functools.partial(layer0_kernel, nt),
        grid=(nc, nt),
        in_specs=[pl.BlockSpec((tm, d), row)] * 2 + [pl.BlockSpec((tm, fc), tile)] * 2 + [pl.BlockSpec((fc, d), chunk)],
        out_specs=[pl.BlockSpec((d, fc), col)] * 2 + [pl.BlockSpec((fc, d), chunk)],
        out_shape=[jax.ShapeDtypeStruct((d, ff), BF16)] * 2 + [jax.ShapeDtypeStruct((ff, d), BF16)],
        scratch_shapes=[pltpu.VMEM((d, fc), F32), pltpu.VMEM((d, fc), F32), pltpu.VMEM((fc, d), F32)],
        compiler_params=params(2),
        cost_estimate=cost(4),
        name="layer0",
    )(a, dy, gate, up, wd)


def adamw(w, m, v, g):
    m = 0.9 * m + 0.1 * g
    v = 0.95 * v + 0.05 * g * g
    step = m * lax.rsqrt(v + 1e-8) + 0.1 * w
    return (w - 0.02 * step).astype(BF16), m, v


def clipped(gradients, sum_of_squares, count):
    factor = jnp.minimum(1.0, 0.5 * lax.rsqrt(sum_of_squares / count + 1e-30))
    return [g * factor for g in gradients]


def solution(mesh):
    reps = mesh.shape["rep"]

    def fetched(block):
        share = block.shape[0] // reps
        mine = lax.dynamic_slice_in_dim(block, lax.axis_index("rep") * share, share, 0)
        return lax.all_gather(mine, ("dp", "rep"), axis=0, tiled=True)

    def step(x, dy, *arrays):
        weights, m, v = (arrays[i : i + 3] for i in (0, 3, 6))
        layers = weights[0].shape[0]
        w = [[fetched(one[number]) for one in weights] for number in range(layers)]
        gate, up, a0, h1, a1 = forward(x[0], *w[0])
        dwg1, dwu1, dwd1, dgate, dup = layer1(a1, dy[0], *w[1])
        scatter = lambda g: lax.psum_scatter(g, "dp", scatter_dimension=0, tiled=True)
        mine1 = [scatter(g) for g in (dwg1, dwu1, dwd1)]
        dy0 = input_grad(dgate, dup, h1, dy[0], w[1][0], w[1][1])
        mine0 = [scatter(g) for g in layer0(a0, dy0, gate, up, w[0][2])]
        gradients = [jnp.stack(pair).astype(F32) for pair in zip(mine0, mine1)]
        squares = lax.psum(sum(jnp.sum(g * g) for g in gradients), "dp")
        gradients = clipped(gradients, squares, lax.psum(1, "dp") * sum(g.size for g in gradients))
        new = [adamw(w.astype(F32), m, v, g) for w, m, v, g in zip(weights, m, v, gradients, strict=True)]
        return tuple(one[which] for which in range(3) for one in new)

    states, cut = P(("rep", "dp"), None, None), P(None, "dp", None)
    return jax.shard_map(
        step,
        mesh=mesh,
        in_specs=(states, states) + (cut,) * 9,
        out_specs=(P("rep", "dp", None),) * 9,
        check_vma=False,
    )
```

time: 711 us -> 913 us (1.28)
  matrix products: 421 us -> 0 us
  waiting for transfers between devices: 194 us -> 570 us
  Pallas kernels: 0 us -> 286 us
  local copies, waits for them, and re-layouts: 28.2 us -> 6.81 us
  other arithmetic: 28.5 us -> 16.7 us
    dot_general x15 -> x0, matrix products: 421 us -> none  [the longest x5 156 us: layer(): gate = jnp.dot(a, w['w_gate'], preferred_element_type=jnp.float32)]
    pallas_call x0 -> x4, Pallas kernels: none -> 286 us  [the longest x1 107 us: layer1(): pl.pallas_call(functools.partial(layer1_kernel, nt), grid=(nc, nt), in_sp...]
    all_gather x6, waiting for transfers between devices: 97.9 us -> 308 us  [fetched(): return lax.all_gather(mine, ('dp', 'rep'), axis=0, tiled=True)]
    reduce_scatter x6, waiting for transfers between devices: 93.9 us -> 259 us  [step(): lax.psum_scatter(g, 'dp', scatter_dimension=0, tiled=True)]
    unnamed x40 -> x26, local copies, waits for them, and re-layouts: 21.8 us -> 1.4 us
  transfers between devices with their start and end apart: 12 -> 12, of which waited for: 9 -> 11; matrix products, arithmetic and copies ran while one was open for 47% -> 1% of each run, Pallas kernels for 0% -> 7%
where the time goes in v1:
time: 913 us; the launch traced here: 912 us
  waiting for transfers between devices  570 us (62%)
  Pallas kernels  286 us (31%)
  between operations  17.1 us (2%)
  other arithmetic  16.7 us (2%)
  blocking collectives  15 us (2%)
    all_gather x6, waiting for transfers between devices, fetched(): return lax.all_gather(mine, ('dp', 'rep'), axis=0, tiled=True)  308 us
    reduce_scatter x6, waiting for transfers between devices, step(): lax.psum_scatter(g, 'dp', scatter_dimension=0, tiled=True)  259 us
    pallas_call x1, Pallas kernels, layer1(): pl.pallas_call(functools.partial(layer1_kernel, nt), grid=(nc, nt), in_sp...  107 us
    pallas_call x1, Pallas kernels, layer0(): pl.pallas_call(functools.partial(layer0_kernel, nt), grid=(nc, nt), in_sp...  73.2 us
    pallas_call x1, Pallas kernels, forward(): pl.pallas_call(functools.partial(forward_kernel, nc, nt), grid=(nc + 1, n...  65.3 us
    pallas_call x1, Pallas kernels, input_grad(): pl.pallas_call(input_grad_kernel, grid=(tokens // tm,), in_specs=[pl.Bloc...  40.3 us
  transfers between devices with their start and end apart: 12, of which 11 were waited for; matrix products, arithmetic and copies ran while one was open for 1% of the time, Pallas kernels for 7%

profile of v1, /device:TPU:0, one launch (start us, length us, event | category | flops | bytes accessed | tf_op | source)
XLA Modules:
  0.0 912.2 jit_solution(16149857549838371592)
XLA Ops:
  7.3 1.3 fusion.29
  13.2 61.6 %all-gather.13.cloned.1.call-done = bf16[1,768,2304]{2,1,0:T(8,128)(2,1)} async-done(((bf16[1,24,2304]{2,1,0:T(8,128)(2,1)}), bf16[1,768,2304]{2,1,0:T(8,128)(2,1)}) %all-gather.13.cloned.1.call-update) | async-done | bytes 3538960 | tf_op jit(solution)/shard_map/all_gather | solution.py:224
  74.8 62.5 %all-gather.15.cloned.1.call-done = bf16[1,768,2304]{2,1,0:T(8,128)(2,1)} async-done(((bf16[1,24,2304]{2,1,0:T(8,128)(2,1)}), bf16[1,768,2304]{2,1,0:T(8,128)(2,1)}) %all-gather.15.cloned.1.call-update) | async-done | bytes 3538960 | tf_op jit(solution)/shard_map/all_gather | solution.py:224
  137.3 62.5 %all-gather.17.cloned.1.call-done = bf16[1,2304,768]{2,1,0:T(8,128)(2,1)} async-done(((bf16[1,72,768]{2,1,0:T(8,128)(2,1)}), bf16[1,2304,768]{2,1,0:T(8,128)(2,1)}) %all-gather.17.cloned.1.call-update) | async-done | bytes 3538960 | tf_op jit(solution)/shard_map/all_gather | solution.py:224
  199.8 65.3 %forward0.1 = (f32[4096,2304]{1,0:T(8,128)}, f32[4096,2304]{1,0:T(8,128)}, bf16[4096,768]{1,0:T(8,128)(2,1)}, bf16[4096,768]{1,0:T(8,128)(2,1)}, bf16[4096,768]{1,0:T(8,128)(2,1)}) custom-call(bf16[4096,768]{1,0:T(8,128)(2,1)} %bitcast.26, bf16[768,2304]{1,0:T(8,128)(2,1)} %bitcast.29, bf16[768,2304]{1,0:T(8,128)(2,1)} %bitcast.32, bf16[2304,768]{1,0:T(8,128)(2,1)} %bitcast.30), custom_call_target="tpu_custom_call" | custom-call | flops 43499999232 | bytes 50000000 | tf_op jit(solution)/shard_map/forward0/pallas_call | solution.py:76
  265.1 59.4 %all-gather.21.cloned.1.call-done = bf16[1,768,2304]{2,1,0:T(8,128)(2,1)} async-done(((bf16[1,24,2304]{2,1,0:T(8,128)(2,1)}), bf16[1,768,2304]{2,1,0:T(8,128)(2,1)}) %all-gather.21.cloned.1.call-update) | async-done | bytes 3538960 | tf_op jit(solution)/shard_map/all_gather | solution.py:224
  324.5 62.3 %all-gather.23.cloned.1.call-done = bf16[1,2304,768]{2,1,0:T(8,128)(2,1)} async-done(((bf16[1,72,768]{2,1,0:T(8,128)(2,1)}), bf16[1,2304,768]{2,1,0:T(8,128)(2,1)}) %all-gather.23.cloned.1.call-update) | async-done | bytes 3538960 | tf_op jit(solution)/shard_map/all_gather | solution.py:224
  386.8 107.0 %layer1.1 = (bf16[768,2304]{1,0:T(8,128)(2,1)}, bf16[768,2304]{1,0:T(8,128)(2,1)}, bf16[2304,768]{1,0:T(8,128)(2,1)}, bf16[4096,2304]{1,0:T(8,128)(2,1)}, bf16[4096,2304]{1,0:T(8,128)(2,1)}) custom-call(bf16[4096,768]{1,0:T(8,128)(2,1)} %get-tuple-element.23.a_ref, bf16[4096,768]{1,0:T(8,128)(2,1)} %bitcast.27, bf16[768,2304]{1,0:T(8,128)(2,1)} %bitcast.33, ...), custom_call_target="tpu_custom_call" | custom-call | flops 86999998464 | bytes 50000000 | tf_op jit(solution)/shard_map/layer1/pallas_call | solution.py:131
  493.8 40.3 %input_grad.1.dy_ref = bf16[4096,768]{1,0:T(8,128)(2,1)} custom-call(bf16[4096,2304]{1,0:T(8,128)(2,1)} %get-tuple-element.24.dgate_ref, bf16[4096,2304]{1,0:T(8,128)(2,1)} %get-tuple-element.25.dup_ref, bf16[4096,768]{1,0:T(8,128)(2,1)} %get-tuple-element.26.h_ref, bf16[4096,768]{1,0:T(8,128)(2,1)} %bitcast.28, bf16[768,2304]{1,0:T(8,128)(2,1)} %bitcast.34, ...), custom_call_target="tpu_custom_call" | custom-call | flops 28999999488 | bytes 50000000 | tf_op jit(solution)/shard_map/input_grad/pallas_call | solution.py:156
  534.1 73.2 %layer0.1 = (bf16[768,2304]{1,0:T(8,128)(2,1)}, bf16[768,2304]{1,0:T(8,128)(2,1)}, bf16[2304,768]{1,0:T(8,128)(2,1)}) custom-call(bf16[4096,768]{1,0:T(8,128)(2,1)} %get-tuple-element.22.a_ref, bf16[4096,768]{1,0:T(8,128)(2,1)} %input_grad.1.dy_ref, f32[4096,2304]{1,0:T(8,128)} %get-tuple-element.27.gate_ref, f32[4096,2304]{1,0:T(8,128)} %get-tuple-element.28.up_ref, ...), custom_call_target="tpu_custom_call" | custom-call | flops 57999998976 | bytes 50000000 | tf_op jit(solution)/shard_map/layer0/pallas_call | solution.py:193
  607.3 0.7 reduce-scatter.9.cloned.1.call-update
  610.7 38.8 %reduce-scatter.7.cloned.1.call-done = bf16[96,2304]{1,0:T(8,128)(2,1)} async-done(((bf16[768,2304]{1,0:T(8,128)(2,1)}), bf16[96,2304]{1,0:T(8,128)(2,1)}) %reduce-scatter.7.cloned.1.call-update) | async-done | bytes 442384 | tf_op jit(solution)/shard_map/reduce_scatter | solution.py:232
  649.5 45.2 %reduce-scatter.9.cloned.1.call-done = bf16[96,2304]{1,0:T(8,128)(2,1)} async-done(((bf16[768,2304]{1,0:T(8,128)(2,1)}), bf16[96,2304]{1,0:T(8,128)(2,1)}) %reduce-scatter.9.cloned.1.call-update) | async-done | bytes 442384 | tf_op jit(solution)/shard_map/reduce_scatter | solution.py:232
  694.7 2.2 fusion.9
  696.9 43.0 %reduce-scatter.11.cloned.1.call-done = bf16[96,2304]{1,0:T(8,128)(2,1)} async-done(((bf16[768,2304]{1,0:T(8,128)(2,1)}), bf16[96,2304]{1,0:T(8,128)(2,1)}) %reduce-scatter.11.cloned.1.call-update) | async-done | bytes 442384 | tf_op jit(solution)/shard_map/reduce_scatter | solution.py:232
  739.9 45.0 %reduce-scatter.13.cloned.1.call-done = bf16[96,2304]{1,0:T(8,128)(2,1)} async-done(((bf16[768,2304]{1,0:T(8,128)(2,1)}), bf16[96,2304]{1,0:T(8,128)(2,1)}) %reduce-scatter.13.cloned.1.call-update) | async-done | bytes 442384 | tf_op jit(solution)/shard_map/reduce_scatter | solution.py:232
  785.0 2.2 fusion.10
  788.5 41.7 %reduce-scatter.15.cloned.1.call-done = bf16[288,768]{1,0:T(8,128)(2,1)} async-done(((bf16[2304,768]{1,0:T(8,128)(2,1)}), bf16[288,768]{1,0:T(8,128)(2,1)}) %reduce-scatter.15.cloned.1.call-update) | async-done | bytes 442384 | tf_op jit(solution)/shard_map/reduce_scatter | solution.py:232
  830.2 45.1 %reduce-scatter.17.cloned.1.call-done = bf16[288,768]{1,0:T(8,128)(2,1)} async-done(((bf16[2304,768]{1,0:T(8,128)(2,1)}), bf16[288,768]{1,0:T(8,128)(2,1)}) %reduce-scatter.17.cloned.1.call-update) | async-done | bytes 442384 | tf_op jit(solution)/shard_map/reduce_scatter | solution.py:232
  875.2 2.2 fusion.11
  878.1 15.0 %psum.7 = f32[]{:T(128)} all-reduce(f32[]{:T(128)S(6)} %add.75), channel_id=1, replica_groups=mesh['rep'=4,'dp'=8] {'dp'}, use_global_device_ids=true, to_apply=%region_9.0 | all-reduce | flops 1 | bytes 8 | tf_op jit(solution)/shard_map/psum | solution.py:237
  893.9 4.5 fusion.17
  899.0 0.8 copy-done.12
  899.8 5.6 fusion.8
  (57 shorter events, 7.7 us)
Async XLA Ops:
  7.2 67.6 %all-gather.13.cloned.1.call-start = ((), (), s32[]{:S(2)}) async-start(), calls=%async_computation.12 | async-start | bytes 3649536 | tf_op jit(solution)/shard_map/all_gather | solution.py:224
  7.2 2.9 copy-start
  9.3 128.0 %all-gather.15.cloned.1.call-start = ((), (), s32[]{:S(2)}) async-start(), calls=%async_computation.13 | async-start | bytes 3649536 | tf_op jit(solution)/shard_map/all_gather | solution.py:224
  10.1 189.7 %all-gather.17.cloned.1.call-start = ((), (), s32[]{:S(2)}) async-start(), calls=%async_computation.14 | async-start | bytes 3649536 | tf_op jit(solution)/shard_map/all_gather | solution.py:224
  10.9 254.2 %all-gather.19.cloned.1.call-start = ((), (), s32[]{:S(2)}) async-start(), calls=%async_computation.15 | async-start | bytes 3649536 | tf_op jit(solution)/shard_map/all_gather | solution.py:224
  11.6 312.8 %all-gather.21.cloned.1.call-start = ((), (), s32[]{:S(2)}) async-start(), calls=%async_computation.16 | async-start | bytes 3649536 | tf_op jit(solution)/shard_map/all_gather | solution.py:224
  12.4 374.4 %all-gather.23.cloned.1.call-start = ((), (), s32[]{:S(2)}) async-start(), calls=%async_computation.17 | async-start | bytes 3649536 | tf_op jit(solution)/shard_map/all_gather | solution.py:224
  13.1 636.4 %reduce-scatter.7.cloned.1.call-start = ((), (), s32[]{:S(2)}) async-start(), calls=%async_computation.6 | async-start | bytes 3981312 | tf_op jit(solution)/shard_map/reduce_scatter | solution.py:232
  607.3 87.4 %reduce-scatter.9.cloned.1.call-start = ((), (), s32[]{:S(2)}) async-start(), calls=%async_computation.7 | async-start | bytes 3981312 | tf_op jit(solution)/shard_map/reduce_scatter | solution.py:232
  608.0 131.9 %reduce-scatter.11.cloned.1.call-start = ((), (), s32[]{:S(2)}) async-start(), calls=%async_computation.8 | async-start | bytes 3981312 | tf_op jit(solution)/shard_map/reduce_scatter | solution.py:232
  608.8 176.2 %reduce-scatter.13.cloned.1.call-start = ((), (), s32[]{:S(2)}) async-start(), calls=%async_computation.9 | async-start | bytes 3981312 | tf_op jit(solution)/shard_map/reduce_scatter | solution.py:232
  609.4 220.8 %reduce-scatter.15.cloned.1.call-start = ((), (), s32[]{:S(2)}) async-start(), calls=%async_computation.10 | async-start | bytes 3981312 | tf_op jit(solution)/shard_map/reduce_scatter | solution.py:232
  610.1 265.1 %reduce-scatter.17.cloned.1.call-start = ((), (), s32[]{:S(2)}) async-start(), calls=%async_computation.11 | async-start | bytes 3981312 | tf_op jit(solution)/shard_map/reduce_scatter | solution.py:232
  610.7 283.1 %copy-start.1 = (bf16[2,288,768]{2,1,0:T(8,128)(2,1)S(1)}, bf16[2,288,768]{2,1,0:T(8,128)(2,1)}, u32[]{:S(2)}) copy-start(bf16[2,288,768]{2,1,0:T(8,128)(2,1)} %param.15) | copy-start | bytes 2654212
  610.7 283.1 %copy-start.5 = (f32[2,288,768]{2,1,0:T(8,128)S(1)}, f32[2,288,768]{2,1,0:T(8,128)}, u32[]{:S(2)}) copy-start(f32[2,288,768]{2,1,0:T(8,128)} %param.21) | copy-start | bytes 5308420
  893.8 4.6 copy-start.2
  893.8 4.6 copy-start.4
  893.8 4.6 copy-start.6
  893.8 4.6 copy-start.7
  893.8 4.6 copy-start.8
  893.9 4.6 copy-start.9
  893.9 4.6 copy-start.10
  893.9 5.1 copy-start.11
  893.9 5.9 copy-start.12
  (1 other events, 2.1 us)
Sparse Core Ops, SparseCore 0:
  11.6 63.1 all-gather.12
  78.3 58.8 all-gather.14
  140.8 58.8 all-gather.16
  203.2 58.8 all-gather.18
  265.5 58.8 all-gather.20
  327.9 58.8 all-gather.22
  607.4 42.0 reduce-scatter.6
  651.8 42.8 reduce-scatter.8
  697.0 42.8 reduce-scatter.10
  742.1 42.8 reduce-scatter.12
  787.3 42.8 reduce-scatter.14
  832.3 42.8 reduce-scatter.16

commit v2 on v1

v2 whole, which is shorter than its diff:
```python
import functools

import jax
import jax.numpy as jnp
from jax import lax
from jax.experimental import pallas as pl
from jax.experimental.pallas import tpu as pltpu
from jax.sharding import PartitionSpec as P

BF16, F32 = jnp.bfloat16, jnp.float32
VMEM_LIMIT = 63 * 2**20
CHIPS = 4
VMEM = pltpu.VMEM
DMA = pltpu.SemaphoreType.DMA


def dot(a, b):
    return jnp.dot(a, b, preferred_element_type=F32)


def dot_t(a, b):
    return lax.dot_general(a, b, (((1,), (1,)), ((), ())), preferred_element_type=F32)


def t_dot(a, b):
    return lax.dot_general(a, b, (((0,), (0,)), ((), ())), preferred_element_type=F32)


def inverse_rms(wide):
    return lax.rsqrt(jnp.mean(wide * wide, -1, keepdims=True) + 1e-6)


def params(dims, **more):
    return pltpu.CompilerParams(dimension_semantics=("arbitrary",) * dims, vmem_limit_bytes=VMEM_LIMIT, **more)


def cost(units):
    return pl.CostEstimate(flops=int(units * 14.5e9), bytes_accessed=50_000_000, transcendentals=0)


def resident(shape):
    return pl.BlockSpec(shape, lambda *_: (0,) * len(shape), pipeline_mode=pl.Buffered(1))


class Place:
    def __init__(self):
        self.me = lax.axis_index("dp")
        self.z, self.core = self.me // 2, self.me % 2
        self.partner = self.me + 1 - 2 * self.core

    def greet(self):
        barrier = pltpu.get_barrier_semaphore()
        signal = lambda to: pl.semaphore_signal(barrier, inc=1, device_id={"dp": to}, device_id_type=pl.DeviceIdType.MESH)
        signal(self.partner)
        pl.when(self.z > 0)(lambda: signal(self.me - 2))
        pl.when(self.z < CHIPS - 1)(lambda: signal(self.me + 2))

    def greeted(self):
        peers = 1 + (self.z + CHIPS - 1) // CHIPS + (2 * CHIPS - 2 - self.z) // CHIPS
        pl.semaphore_wait(pltpu.get_barrier_semaphore(), peers)


def remote(src, dst, send_sem, recv_sem, to):
    return pltpu.make_async_remote_copy(src, dst, send_sem, recv_sem, device_id={"dp": to}, device_id_type=pl.DeviceIdType.MESH)


class Sum:
    def __init__(self, place, own, theirs, arriving, leaving, out, sems):
        self.place, self.own, self.theirs, self.arriving, self.leaving, self.out = place, own, theirs, arriving, leaving, out
        self.half_sems, self.arrive_sems, self.leave_sems = sems
        self.n = own.shape[1]

    @staticmethod
    def scratch(n, share, d):
        return [
            VMEM((n, CHIPS, share, d), BF16),
            VMEM((2, 3, n, share, d), BF16),
            VMEM((2, 3, n, share, d), BF16),
            DMA((2,)),
            DMA((2, 3, n)),
            DMA((2, 3, n)),
        ]

    @staticmethod
    def on(place, own, out, scratch):
        theirs, arriving, leaving, *sems = scratch
        return Sum(place, own, theirs, arriving, leaving, out, sems)

    def halves(self):
        p = self.place
        return remote(self.own.at[1 - p.core], self.theirs, self.half_sems.at[0], self.half_sems.at[1], p.partner)

    def copy(self, way, k, m):
        to = self.place.me + (2, -2)[way]
        return remote(self.leaving.at[way, k, m], self.arriving.at[way, k, m], self.leave_sems.at[way, k, m], self.arrive_sems.at[way, k, m], to)

    def mine(self, m, chip):
        return self.own[self.place.core, m, chip].astype(F32) + self.theirs[m, chip].astype(F32)

    def send(self, k, m):
        z = self.place.z
        for way, behind, chip in ((0, z, 3 + z - k), (1, 3 - z, z - 3 + k)):

            @pl.when((behind <= k) & (behind < 3))
            def _(way=way, behind=behind, chip=chip):
                before = (k + 2) % 3

                @pl.when(behind > 0)
                def _():
                    self.copy(way, before, m).wait_recv()

                total = self.mine(m, chip) + jnp.where(behind > 0, self.arriving[way, before, m].astype(F32), 0.0)
                self.leaving[way, k, m] = total.astype(BF16)
                self.copy(way, k, m).start()

    def finish(self, m):
        z = self.place.z
        pl.when(z > 0)(lambda: self.copy(0, 2, m).wait_recv())
        pl.when(z < 3)(lambda: self.copy(1, 2, m).wait_recv())
        total = self.mine(m, z)
        for way, there in ((0, z > 0), (1, z < 3)):
            total += jnp.where(there, self.arriving[way, 2, m].astype(F32), 0.0)
        self.out[m] = total.astype(BF16)

    def tick(self, i):
        k, m = i // self.n, i % self.n
        pl.when(k < 3)(lambda: self.send(k, m))
        pl.when(k == 3)(lambda: self.finish(m))

    def drain(self):
        z = self.place.z
        for way, behind in ((0, z), (1, 3 - z)):
            for k in range(3):

                @pl.when((behind <= k) & (behind < 3))
                def _(way=way, k=k):
                    for m in range(self.n):
                        self.copy(way, k, m).wait_send()


def keep(own, m, acc):
    share = acc.shape[0] // (2 * CHIPS)
    for chip in range(CHIPS):
        for core in range(2):
            at = (2 * chip + core) * share
            own[core, m, chip] = acc[at : at + share, :].astype(BF16)


def forward_kernel(nc, nt, x_ref, wg_ref, wu_ref, wd_ref, gate_ref, up_ref, hid_out, a_out, h_out, a1_out, a_s, hid_s):
    c, t = pl.program_id(0), pl.program_id(1)
    tm = x_ref.shape[0]
    fc = wg_ref.shape[1]
    rows = pl.ds(pl.multiple_of(t * tm, tm), tm)

    @pl.when(c == 0)
    def _():
        wide = x_ref[...].astype(F32)
        a = (wide * inverse_rms(wide)).astype(BF16)
        a_s[rows, :] = a
        a_out[...] = a

    for k in range(nc):
        @pl.when(c == k)
        def _(k=k):
            a = a_s[rows, :]
            gate, up = dot(a, wg_ref[...]), dot(a, wu_ref[...])
            gate_ref[...] = gate
            up_ref[...] = up
            hid = (gate * jax.nn.sigmoid(gate) * up).astype(BF16)
            hid_s[rows, k * fc : (k + 1) * fc] = hid
            hid_out[...] = hid

    @pl.when(c == nc)
    def _():
        h = x_ref[...] + dot(hid_s[rows, :], wd_ref[...]).astype(BF16)
        h_out[...] = h
        wide = h.astype(F32)
        a1_out[...] = (wide * inverse_rms(wide)).astype(BF16)


def forward(x, wg, wu, wd, tm=512, fc=768):
    tokens, d = x.shape
    ff = wg.shape[1]
    nc, nt = ff // fc, tokens // tm
    col = lambda c, t: (0, jnp.minimum(c, nc - 1))
    tile = lambda c, t: (jnp.where(c == nc, nt - 1, t), jnp.minimum(c, nc - 1))
    first = lambda c, t: (jnp.where(c == 0, t, nt - 1), 0)
    last = lambda c, t: (jnp.where(c == nc, t, 0), 0)
    return pl.pallas_call(
        functools.partial(forward_kernel, nc, nt),
        grid=(nc + 1, nt),
        in_specs=[
            pl.BlockSpec((tm, d), lambda c, t: (jnp.where((c == 0) | (c == nc), t, nt - 1), 0)),
            pl.BlockSpec((d, fc), col),
            pl.BlockSpec((d, fc), col),
            resident((ff, d)),
        ],
        out_specs=[pl.BlockSpec((tm, fc), tile)] * 3 + [pl.BlockSpec((tm, d), first), pl.BlockSpec((tm, d), last), pl.BlockSpec((tm, d), last)],
        out_shape=[jax.ShapeDtypeStruct((tokens, ff), F32)] * 2
        + [jax.ShapeDtypeStruct((tokens, ff), BF16)]
        + [jax.ShapeDtypeStruct((tokens, d), BF16)] * 3,
        scratch_shapes=[VMEM((tokens, d), BF16), VMEM((tokens, ff), BF16)],
        compiler_params=params(2),
        cost_estimate=cost(3),
        name="forward0",
    )(x, wg, wu, wd)


def hidden_grads(gate, up, dhid):
    dhid = dhid.astype(BF16).astype(F32)
    sig = jax.nn.sigmoid(gate)
    silu = gate * sig
    hid = (silu * up).astype(BF16)
    dup = (dhid * silu).astype(BF16)
    dgate = (dhid * up * (sig * (1 + gate * (1 - sig)))).astype(BF16)
    return hid, dgate, dup


def layer1_kernel(nc, nt, a_ref, dy_ref, wg_ref, wu_ref, wd_ref, dgate_ref, dup_ref, own_ref, sum_ref, acg, acu, acd, *scratch):
    c, t = pl.program_id(0), pl.program_id(1)
    place = Place()
    half = len(scratch) // 2
    sums = [Sum.on(place, own_ref, sum_ref.at[g], scratch[g * half : (g + 1) * half]) for g in range(2)]

    def tick(j):
        for g, one in enumerate(sums):
            @pl.when(c == g + 1)
            def _(one=one):
                if j == 0:
                    pl.when(t == 0)(lambda: one.halves().wait())
                one.tick(3 * t + j)

    @pl.when((c == 0) & (t == 0))
    def _():
        place.greet()

    @pl.when((c == 0) & (t == 1))
    def _():
        place.greeted()

    @pl.when(t == 0)
    def _():
        for acc in (acg, acu, acd):
            acc[...] = jnp.zeros_like(acc)

    a, dy = a_ref[...], dy_ref[...]
    gate, up = dot(a, wg_ref[...]), dot(a, wu_ref[...])
    tick(0)
    hid, dgate, dup = hidden_grads(gate, up, dot_t(dy, wd_ref[...]))
    dgate_ref[...] = dgate
    dup_ref[...] = dup
    tick(1)
    acd[...] += t_dot(hid, dy)
    acg[...] += t_dot(a, dgate)
    tick(2)
    acu[...] += t_dot(a, dup)

    @pl.when(t == nt - 1)
    def _():
        for m, acc in enumerate((acg, acu, acd)):
            keep(own_ref, m, acc)
        for g, one in enumerate(sums):
            @pl.when(c == g)
            def _(g=g, one=one):
                one.halves().start()

            pl.when(c == g + 1)(one.drain)


def layer1(a, dy, wg, wu, wd, tm=1024, fc=768):
    tokens, d = a.shape
    ff = wg.shape[1]
    nc, nt = ff // fc, tokens // tm
    share = d // (2 * CHIPS)
    row, col, chunk, tile = (lambda c, t: (t, 0)), (lambda c, t: (0, c)), (lambda c, t: (c, 0)), (lambda c, t: (t, c))
    own, out = (2, 3, CHIPS, share, d), (2, 3, share, d)
    return pl.pallas_call(
        functools.partial(layer1_kernel, nc, nt),
        grid=(nc, nt),
        in_specs=[pl.BlockSpec((tm, d), row)] * 2 + [pl.BlockSpec((d, fc), col)] * 2 + [pl.BlockSpec((fc, d), chunk)],
        out_specs=[pl.BlockSpec((tm, fc), tile)] * 2 + [resident(own), resident(out)],
        out_shape=[jax.ShapeDtypeStruct((tokens, ff), BF16)] * 2 + [jax.ShapeDtypeStruct(own, BF16), jax.ShapeDtypeStruct(out, BF16)],
        scratch_shapes=[VMEM((d, fc), F32), VMEM((d, fc), F32), VMEM((fc, d), F32)] + Sum.scratch(3, share, d) * 2,
        compiler_params=params(2, collective_id=1, has_side_effects=True),
        cost_estimate=cost(6),
        name="layer1",
    )(a, dy, wg, wu, wd)


def between_kernel(nt, dgate_ref, dup_ref, h_ref, dy_ref, hid_ref, wg_ref, wu_ref, own_in, out_ref, own_ref, sum_ref, acd, *scratch):
    t = pl.program_id(0)
    place = Place()
    one = Sum.on(place, own_in, sum_ref, scratch)

    @pl.when(t == 0)
    def _():
        place.greet()
        acd[...] = jnp.zeros_like(acd)

    @pl.when(t == 1)
    def _():
        place.greeted()
        one.halves().start()

    def tick(j):
        @pl.when(t >= 2)
        def _():
            if j == 0:
                pl.when(t == 2)(lambda: one.halves().wait())
            one.tick(2 * (t - 2) + j)

    tick(0)
    dn = (dot_t(dgate_ref[...], wg_ref[...]) + dot_t(dup_ref[...], wu_ref[...])).astype(BF16).astype(F32)
    wide = h_ref[...].astype(F32)
    scale = inverse_rms(wide)
    along = jnp.sum(dn * wide, -1, keepdims=True) * (scale * scale * scale) * (1.0 / wide.shape[-1])
    dy = dy_ref[...] + (dn * scale - wide * along).astype(BF16)
    out_ref[...] = dy
    tick(1)
    acd[...] += t_dot(hid_ref[...], dy)

    @pl.when(t == nt - 1)
    def _():
        one.drain()
        rows = acd.shape[0] // 3
        for c in range(3):
            keep(own_ref, c, acd[c * rows : (c + 1) * rows, :])


def between(dgate, dup, h, dy, hid, wg, wu, own, tm=512):
    tokens, d = h.shape
    ff = wg.shape[1]
    share = d // (2 * CHIPS)
    nt = tokens // tm
    assert nt == 8
    row = lambda t: (t, 0)
    out = (3, share, d)
    return pl.pallas_call(
        functools.partial(between_kernel, nt),
        grid=(nt,),
        in_specs=[pl.BlockSpec((tm, ff), row)] * 2 + [pl.BlockSpec((tm, d), row)] * 2 + [pl.BlockSpec((tm, ff), row)] + [resident((d, ff))] * 2 + [resident(own.shape)],
        out_specs=[pl.BlockSpec((tm, d), row), resident(own.shape), resident(out)],
        out_shape=[jax.ShapeDtypeStruct((tokens, d), BF16), jax.ShapeDtypeStruct(own.shape, BF16), jax.ShapeDtypeStruct(out, BF16)],
        scratch_shapes=[VMEM((ff, d), F32)] + Sum.scratch(3, share, d),
        compiler_params=params(1, collective_id=2, has_side_effects=True),
        cost_estimate=cost(3),
        name="between",
    )(dgate, dup, h, dy, hid, wg, wu, own)


def layer0_kernel(nt, a_ref, dy_ref, gate_ref, up_ref, wd_ref, own_in, own_ref, sum0_ref, sum1_ref, acg, acu, own1, *scratch):
    c, t = pl.program_id(0), pl.program_id(1)
    place = Place()
    half = len(scratch) // 2
    first = Sum.on(place, own_in, sum0_ref, scratch[:half])
    second = Sum.on(place, own1, sum1_ref, scratch[half:])
    step = c * nt + t

    @pl.when(step == 0)
    def _():
        place.greet()

    @pl.when(step == 1)
    def _():
        place.greeted()
        first.halves().start()

    @pl.when(t == 0)
    def _():
        for acc in (acg, acu):
            acc[...] = jnp.zeros_like(acc)

    @pl.when((step >= 2) & (step < 14))
    def _():
        pl.when(step == 2)(lambda: first.halves().wait())
        first.tick(step - 2)

    @pl.when((step >= 14) & (step < 22))
    def _():
        pl.when(step == 14)(lambda: second.halves().wait())
        second.tick(step - 14)

    a, dy = a_ref[...], dy_ref[...]
    _, dgate, dup = hidden_grads(gate_ref[...], up_ref[...], dot_t(dy, wd_ref[...]))
    acg[...] += t_dot(a, dgate)
    acu[...] += t_dot(a, dup)

    @pl.when(t == nt - 1)
    def _():
        for m, acc in enumerate((acg, acu)):
            pl.when(c == 0)(lambda m=m, acc=acc: keep(own1, m, acc))
            pl.when(c == 1)(lambda m=m, acc=acc: keep(own_ref, m, acc))
            pl.when(c == 2)(lambda m=m, acc=acc: keep(own_ref, 2 + m, acc))
        pl.when(c == 0)(lambda: second.halves().start())

        @pl.when(c == 2)
        def _():
            first.drain()
            second.drain()


def layer0(a, dy, gate, up, wd, own, tm=512, fc=768):
    tokens, d = a.shape
    ff = wd.shape[0]
    nc, nt = ff // fc, tokens // tm
    share = d // (2 * CHIPS)
    row, chunk, tile = (lambda c, t: (t, 0)), (lambda c, t: (c, 0)), (lambda c, t: (t, c))
    rest, out0, out1 = (2, 4, CHIPS, share, d), (3, share, d), (2, share, d)
    return pl.pallas_call(
        functools.partial(layer0_kernel, nt),
        grid=(nc, nt),
        in_specs=[pl.BlockSpec((tm, d), row)] * 2 + [pl.BlockSpec((tm, fc), tile)] * 2 + [pl.BlockSpec((fc, d), chunk), resident(own.shape)],
        out_specs=[resident(rest), resident(out0), resident(out1)],
        out_shape=[jax.ShapeDtypeStruct(rest, BF16), jax.ShapeDtypeStruct(out0, BF16), jax.ShapeDtypeStruct(out1, BF16)],
        scratch_shapes=[VMEM((d, fc), F32), VMEM((d, fc), F32), VMEM((2, 2, CHIPS, share, d), BF16)] + Sum.scratch(3, share, d) + Sum.scratch(2, share, d),
        compiler_params=params(2, collective_id=3, has_side_effects=True),
        cost_estimate=cost(3),
        name="layer0",
    )(a, dy, gate, up, wd, own)


def rest_kernel(own_in, sum_ref, *scratch):
    place = Place()
    one = Sum.on(place, own_in, sum_ref, scratch)
    place.greet()
    place.greeted()
    one.halves().start()
    one.halves().wait()

    @pl.loop(0, 4 * one.n)
    def _(i):
        one.tick(i)

    one.drain()


def rest(own):
    _, n, _, share, d = own.shape
    return pl.pallas_call(
        rest_kernel,
        in_specs=[pl.BlockSpec(memory_space=VMEM)],
        out_specs=pl.BlockSpec(memory_space=VMEM),
        out_shape=jax.ShapeDtypeStruct((n, share, d), BF16),
        scratch_shapes=Sum.scratch(n, share, d),
        compiler_params=pltpu.CompilerParams(vmem_limit_bytes=VMEM_LIMIT, collective_id=4, has_side_effects=True),
        cost_estimate=cost(3),
        name="rest",
    )(own)


def adamw(w, m, v, g):
    m = 0.9 * m + 0.1 * g
    v = 0.95 * v + 0.05 * g * g
    step = m * lax.rsqrt(v + 1e-8) + 0.1 * w
    return (w - 0.02 * step).astype(BF16), m, v


def clipped(gradients, sum_of_squares, count):
    factor = jnp.minimum(1.0, 0.5 * lax.rsqrt(sum_of_squares / count + 1e-30))
    return [g * factor for g in gradients]


def solution(mesh):
    n = mesh.shape["dp"]

    def whole(wg, wu, wd):
        share = wg.shape[0]
        columns = lambda w: lax.all_gather(w.reshape(share, n, 3, share).transpose(0, 2, 1, 3).reshape(share, -1), "dp", axis=0, tiled=True)
        rows = lax.all_gather(wd.reshape(3, share, -1), "dp", axis=1, tiled=True).reshape(-1, wd.shape[1])
        return columns(wg), columns(wu), rows

    def natural(chunks):
        share = chunks.shape[1]
        return chunks.reshape(3, share, n, share).transpose(1, 2, 0, 3).reshape(share, -1)

    def step(x, dy, *arrays):
        weights, m, v = (arrays[i : i + 3] for i in (0, 3, 6))
        w0, w1 = (whole(*(one[number] for one in weights)) for number in range(2))
        gate, up, hid, a0, h1, a1 = forward(x[0], *w0)
        dgate, dup, own, first = layer1(a1, dy[0], *w1)
        dy0, own, second = between(dgate, dup, h1, dy[0], hid, w1[0], w1[1], own)
        own, down0, third = layer0(a0, dy0, gate, up, w0[2], own)
        last = rest(own)
        one = jnp.concatenate([first, second[None]])
        mine1 = [natural(one[:, 0]), natural(one[:, 1]), one[:, 2].reshape(-1, one.shape[-1])]
        pair = jnp.concatenate([third[None], last.reshape(2, 2, *last.shape[1:])])
        mine0 = [natural(pair[:, 0]), natural(pair[:, 1]), down0.reshape(-1, down0.shape[-1])]
        gradients = [jnp.stack(both).astype(F32) for both in zip(mine0, mine1)]
        squares = lax.psum(sum(jnp.sum(g * g) for g in gradients), "dp")
        gradients = clipped(gradients, squares, n * sum(g.size for g in gradients))
        new = [adamw(w.astype(F32), m, v, g) for w, m, v, g in zip(weights, m, v, gradients, strict=True)]
        return tuple(one[which] for which in range(3) for one in new)

    states, cut = P(("rep", "dp"), None, None), P(None, "dp", None)
    return jax.shard_map(
        step,
        mesh=mesh,
        in_specs=(states, states) + (cut,) * 9,
        out_specs=(P("rep", "dp", None),) * 9,
        check_vma=False,
    )
```

time: 913 us -> 676 us (0.74)
  waiting for transfers between devices: 570 us -> 170 us
  Pallas kernels: 286 us -> 399 us
  local copies, waits for them, and re-layouts: 6.81 us -> 43 us
    reduce_scatter x6 -> x0, waiting for transfers between devices: 259 us -> none  [step(): lax.psum_scatter(g, 'dp', scatter_dimension=0, tiled=True)]
    all_gather x6, waiting for transfers between devices: 308 us -> 170 us  [the longest x4 84.8 us: whole(): lax.all_gather(w.reshape(share, n, 3, share).transpose(0, 2, 1, 3).reshap...]
    pallas_call x2 -> x3, Pallas kernels: 147 us -> 257 us  [the longest x1 126 us: layer1(): pl.pallas_call(functools.partial(layer1_kernel, nc, nt), grid=(nc, nt), i...]
    unnamed x26 -> x56, local copies, waits for them, and re-layouts: 1.4 us -> 28.1 us
  transfers between devices with their start and end apart: 12 -> 6, of which waited for: 11 -> 5; matrix products, arithmetic and copies ran while one was open for 1% -> 2% of each run, Pallas kernels for 7% -> 10%
where the time goes in v2:
time: 676 us; the launch traced here: 669 us
  Pallas kernels  399 us (59%)
  waiting for transfers between devices  170 us (25%)
  local copies, waits for them, and re-layouts  43 us (6%)
  other arithmetic  22.3 us (3%)
  between operations  18 us (3%)
  blocking collectives  16 us (2%)
    pallas_call x1, Pallas kernels, layer1(): pl.pallas_call(functools.partial(layer1_kernel, nc, nt), grid=(nc, nt), i...  126 us
    all_gather x4, waiting for transfers between devices, whole(): lax.all_gather(w.reshape(share, n, 3, share).transpose(0, 2, 1, 3).reshap...  84.8 us
    all_gather x2, waiting for transfers between devices, whole(): lax.all_gather(wd.reshape(3, share, -1), 'dp', axis=1, tiled=True)  84.8 us
    pallas_call x1, Pallas kernels, between(): pl.pallas_call(functools.partial(between_kernel, nt), grid=(nt,), in_spec...  81.4 us
    pallas_call x1, Pallas kernels, layer0(): pl.pallas_call(functools.partial(layer0_kernel, nt), grid=(nc, nt), in_sp...  73.2 us
    pallas_call x1, Pallas kernels, forward(): pl.pallas_call(functools.partial(forward_kernel, nc, nt), grid=(nc + 1, n...  69 us
    pallas_call x1, Pallas kernels, rest(): pl.pallas_call(rest_kernel, in_specs=[pl.BlockSpec(memory_space=VMEM)], o...  48.8 us
    unnamed x56, local copies, waits for them, and re-layouts  28.1 us
  transfers between devices with their start and end apart: 6, of which 5 were waited for; matrix products, arithmetic and copies ran while one was open for 2% of the time, Pallas kernels for 10%

profile of v2, /device:TPU:0, one launch (start us, length us, event | category | flops | bytes accessed | tf_op | source)
XLA Modules:
  0.0 668.7 jit_solution(10173962299102422972)
XLA Ops:
  21.0 3.0 copy.68
  24.0 1.9 copy.69
  25.9 1.9 copy.51
  27.8 26.7 %all-gather.7.cloned.1.call-done.wg_ref = bf16[768,2304]{1,0:T(8,128)(2,1)} async-done(((bf16[96,2304]{1,0:T(8,128)(2,1)}), bf16[768,2304]{1,0:T(8,128)(2,1)}) %all-gather.7.cloned.1.call-update) | async-done | bytes 3538960 | tf_op jit(solution)/shard_map/all_gather | solution.py:468
  54.6 42.5 %all-gather.9.cloned.1.call-done.wu_ref = bf16[768,2304]{1,0:T(8,128)(2,1)} async-done(((bf16[96,2304]{1,0:T(8,128)(2,1)}), bf16[768,2304]{1,0:T(8,128)(2,1)}) %all-gather.9.cloned.1.call-update) | async-done | bytes 3538960 | tf_op jit(solution)/shard_map/all_gather | solution.py:468
  97.1 42.5 %all-gather.11.cloned.1.call-done = bf16[3,768,768]{2,1,0:T(8,128)(2,1)} async-done(((bf16[3,96,768]{2,1,0:T(8,128)(2,1)}), bf16[3,768,768]{2,1,0:T(8,128)(2,1)}) %all-gather.11.cloned.1.call-update) | async-done | bytes 3538960 | tf_op jit(solution)/shard_map/all_gather | solution.py:469
  139.5 69.0 %forward0.1 = (f32[4096,2304]{1,0:T(8,128)}, f32[4096,2304]{1,0:T(8,128)}, bf16[4096,2304]{1,0:T(8,128)(2,1)}, bf16[4096,768]{1,0:T(8,128)(2,1)}, bf16[4096,768]{1,0:T(8,128)(2,1)}, /*index=5*/bf16[4096,768]{1,0:T(8,128)(2,1)}) custom-call(bf16[4096,768]{1,0:T(8,128)(2,1)} %bitcast.78, bf16[768,2304]{1,0:T(8,128)(2,1)} %all-gather.7.cloned.1.call-done.wg_ref, ...), custom_call_target="tpu_custom_call" | custom-call | flops 43499999232 | bytes 50000000 | tf_op jit(solution)/shard_map/forward0/pallas_call | solution.py:189
  208.5 15.6 %all-gather.15.cloned.1.call-done.wu_ref = bf16[768,2304]{1,0:T(8,128)(2,1)} async-done(((bf16[96,2304]{1,0:T(8,128)(2,1)}), bf16[768,2304]{1,0:T(8,128)(2,1)}) %all-gather.15.cloned.1.call-update) | async-done | bytes 3538960 | tf_op jit(solution)/shard_map/all_gather | solution.py:468
  224.2 42.3 %all-gather.17.cloned.1.call-done = bf16[3,768,768]{2,1,0:T(8,128)(2,1)} async-done(((bf16[3,96,768]{2,1,0:T(8,128)(2,1)}), bf16[3,768,768]{2,1,0:T(8,128)(2,1)}) %all-gather.17.cloned.1.call-update) | async-done | bytes 3538960 | tf_op jit(solution)/shard_map/all_gather | solution.py:469
  266.5 126.4 %layer1.1 = (bf16[4096,2304]{1,0:T(8,128)(2,1)}, bf16[4096,2304]{1,0:T(8,128)(2,1)}, bf16[2,3,4,96,768]{4,3,2,1,0:T(8,128)(2,1)}, bf16[2,3,96,768]{3,2,1,0:T(8,128)(2,1)}) custom-call(bf16[4096,768]{1,0:T(8,128)(2,1)} %get-tuple-element.26.a_ref, bf16[4096,768]{1,0:T(8,128)(2,1)} %bitcast.79, bf16[768,2304]{1,0:T(8,128)(2,1)} %all-gather.13.cloned.1.call-done.wg_ref, ...), custom_call_target="tpu_custom_call" | custom-call | flops 86999998464 | bytes 50000000 | tf_op jit(solution)/shard_map/layer1/pallas_call | solution.py:277
  392.9 81.4 %between.1 = (bf16[4096,768]{1,0:T(8,128)(2,1)}, bf16[2,3,4,96,768]{4,3,2,1,0:T(8,128)(2,1)}, bf16[3,96,768]{2,1,0:T(8,128)(2,1)}) custom-call(bf16[4096,2304]{1,0:T(8,128)(2,1)} %get-tuple-element.27.dgate_ref, bf16[4096,2304]{1,0:T(8,128)(2,1)} %get-tuple-element.28.dup_ref, bf16[4096,768]{1,0:T(8,128)(2,1)} %get-tuple-element.29.h_ref, ...), custom_call_target="tpu_custom_call" | custom-call | flops 43499999232 | bytes 50000000 | tf_op jit(solution)/shard_map/between/pallas_call | solution.py:338
  474.3 73.2 %layer0.1 = (bf16[2,4,4,96,768]{4,3,2,1,0:T(8,128)(2,1)}, bf16[3,96,768]{2,1,0:T(8,128)(2,1)}, bf16[2,96,768]{2,1,0:T(8,128)(2,1)}) custom-call(bf16[4096,768]{1,0:T(8,128)(2,1)} %get-tuple-element.25.a_ref, bf16[4096,768]{1,0:T(8,128)(2,1)} %get-tuple-element.32.dy_ref, f32[4096,2304]{1,0:T(8,128)} %get-tuple-element.33.gate_ref, ...), custom_call_target="tpu_custom_call" | custom-call | flops 43499999232 | bytes 50000000 | tf_op jit(solution)/shard_map/layer0/pallas_call | solution.py:409
  547.6 48.8 %rest.1 = bf16[4,96,768]{2,1,0:T(8,128)(2,1)} custom-call(bf16[2,4,4,96,768]{4,3,2,1,0:T(8,128)(2,1)} %get-tuple-element.37.own_in), custom_call_target="tpu_custom_call" | custom-call | flops 43499999232 | bytes 50000000 | tf_op jit(solution)/shard_map/rest/pallas_call | solution.py:439
  599.7 2.2 pad_maximum_fusion.3
  605.3 2.3 fusion.16
  611.5 3.0 copy.66
  614.5 16.0 %psum.7 = f32[]{:T(128)} all-reduce(f32[]{:T(128)S(6)} %add.51), channel_id=1, replica_groups=mesh['rep'=4,'dp'=8] {'dp'}, use_global_device_ids=true, to_apply=%region_3.0 | all-reduce | flops 1 | bytes 8 | tf_op jit(solution)/shard_map/psum | solution.py:489
  631.2 5.3 fusion.11
  636.5 2.9 copy.73
  639.5 3.1 copy.75
  642.5 2.3 copy.71
  644.8 5.3 fusion.6
  650.2 3.1 copy.72
  656.8 4.6 fusion.19
  (82 shorter events, 25.3 us)
Async XLA Ops:
  7.2 47.4 %all-gather.7.cloned.1.call-start = ((), (), s32[]{:S(2)}) async-start(), calls=%async_computation | async-start | bytes 3981312 | tf_op jit(solution)/shard_map/all_gather | solution.py:468
  10.6 86.5 %all-gather.9.cloned.1.call-start = ((), (), s32[]{:S(2)}) async-start(), calls=%async_computation.1 | async-start | bytes 3981312 | tf_op jit(solution)/shard_map/all_gather | solution.py:468
  12.3 3.8 copy-start.2
  12.3 3.8 copy-start.14
  16.1 2.8 copy-start.16
  16.1 123.4 %all-gather.11.cloned.1.call-start = ((), (), s32[]{:S(2)}) async-start(), calls=%async_computation.2 | async-start | bytes 3981312 | tf_op jit(solution)/shard_map/all_gather | solution.py:469
  17.1 191.4 %all-gather.13.cloned.1.call-start = ((), (), s32[]{:S(2)}) async-start(), calls=%async_computation.3 | async-start | bytes 3981312 | tf_op jit(solution)/shard_map/all_gather | solution.py:468
  18.8 205.4 %all-gather.15.cloned.1.call-start = ((), (), s32[]{:S(2)}) async-start(), calls=%async_computation.4 | async-start | bytes 3981312 | tf_op jit(solution)/shard_map/all_gather | solution.py:468
  20.4 3.6 copy-start.17
  20.4 246.1 %all-gather.17.cloned.1.call-start = ((), (), s32[]{:S(2)}) async-start(), calls=%async_computation.5 | async-start | bytes 3981312 | tf_op jit(solution)/shard_map/all_gather | solution.py:469
  24.0 1.9 copy-start.18
  547.6 48.9 %copy-start.21 = (bf16[2,96,768]{2,1,0:T(8,128)(2,1)S(1)}, bf16[2,96,768]{2,1,0:T(8,128)(2,1)}, u32[]{:S(2)}) copy-start(bf16[2,96,768]{2,1,0:T(8,128)(2,1)} %get-tuple-element.36) | copy-start | bytes 884740
  597.5 2.2 copy-start.20
  598.6 9.0 %copy-start.7 = (bf16[96,8,3,96]{0,3,2,1:T(8,128)(2,1)}, bf16[96,8,3,96]{0,3,2,1:T(8,128)(2,1)S(1)}, u32[]{:S(2)}) copy-start(bf16[96,8,3,96]{0,3,2,1:T(8,128)(2,1)S(1)} %copy.62) | copy-start | bytes 1327108
  599.7 8.0 %copy-start.9 = (bf16[96,8,3,96]{0,3,2,1:T(8,128)(2,1)}, bf16[96,8,3,96]{0,3,2,1:T(8,128)(2,1)S(1)}, u32[]{:S(2)}) copy-start(bf16[96,8,3,96]{0,3,2,1:T(8,128)(2,1)S(1)} %copy.64) | copy-start | bytes 1327108
  602.0 5.7 copy-start.12
  603.0 4.6 copy-start.8
  605.3 2.3 copy-start.10
  609.1 22.1 %copy-start.3 = (bf16[2,96,2304]{1,2,0:T(8,128)(2,1)S(1)}, bf16[2,96,2304]{1,2,0:T(8,128)(2,1)}, u32[]{:S(2)}) copy-start(bf16[2,96,2304]{1,2,0:T(8,128)(2,1)} %copy-done.2) | copy-start | bytes 2654212
  609.1 22.1 %copy-start.5 = (f32[2,96,2304]{1,2,0:T(8,128)S(1)}, f32[2,96,2304]{1,2,0:T(8,128)}, u32[]{:S(2)}) copy-start(f32[2,96,2304]{1,2,0:T(8,128)} %copy.68) | copy-start | bytes 5308420
  639.5 5.4 copy-start.1
  639.5 5.4 copy-start.4
  650.2 3.1 copy-start.6
  653.2 1.8 copy-start.11
  (4 other events, 6.2 us)
Sparse Core Ops, SparseCore 0:
  10.7 43.8 all-gather.6
  56.8 40.2 all-gather.8
  99.2 40.2 all-gather.10
  141.6 40.2 all-gather.12
  183.9 40.2 all-gather.14
  226.2 40.2 all-gather.16
